TPU v7x, 512 devices: a 8x2x16 block of a 8x8x16 slice. The times are simulated.
512 devices in a mesh: groups: 2 (over y), ctx: 16 (over z), seq: 8 (over x), head: 2 (over core).
Axes of the slice: x: 8, y: 2, z: 16, core: 2. Of those that a mesh axis runs over, the one named last changes fastest.
The devices are a block of a 8x8x16 slice.
Arguments:
- queries: bfloat16 [16, 4, 128, 576], P(('groups', 'seq'), None, ('ctx', 'head')), parts along dimension 0, may hold values from -36 to 36
- cache: bfloat16 [16, 49152, 576], P(('groups', 'seq'), 'ctx'), parts along dimension 0, may hold values from -8 to 8
- lengths: int32 [16], P(('groups', 'seq')), parts along dimension 0, may hold values from 12288 to 49152, as said below
- offsets: int32 [16, 4], P(('groups', 'seq')), parts along dimension 0, may hold values from 0 to 3
- w_uv: bfloat16 [128, 512, 128], P(('ctx', 'head')), may hold values from -0.25 to 0.25
- w_out: bfloat16 [16384, 7168], P(('ctx', 'head'), 'seq'), may hold values from -0.046875 to 0.046875
Outputs:
- mixed: bfloat16 [64, 7168], P(('groups', 'ctx', 'head'), 'seq'), parts along dimension 0
There are 2 independent parts, one for each index of `groups`. A program takes and returns all parts, laid end to end along the dimension named above; an argument that names none is the same for every part. Nothing has to cross between parts.
Inputs may be any that keep to these rules, and one draw needn't show every extreme that they name: `lengths`: each sequence's filled length, its 4 draft tokens included; some sequence reaches 49152 in every draw. Draft token t of sequence s sits at position lengths[s] - 4 + offsets[s, t].
All inputs are finite; a program needn't handle non-finite values.
Results may differ from a plain program's by a relative error of at most 0.014.
Values may be sent and summed in bfloat16 or wider, within the bound.
No kernel may reach another device: no remote copies, remote signals or barrier semaphores. Data moves between devices by JAX's collectives and lax.ppermute only.
A program may use at most 64 MiB of HBM per device.

v0:
```python
import math
import jax
import jax.numpy as jnp
from jax import lax
from jax.sharding import PartitionSpec as P

LATENT = 512
ROPE = 64
NOPE = 128
DRAFT = 4
theta = 10000.0
negative = -1e30


def copy_for_each(value, axis):
    devices = lax.axis_size(axis)
    return lax.all_to_all(
        jnp.broadcast_to(value[None], (devices, *value.shape)), axis, 0, 0, tiled=True
    )


def taken_together(value, axis):
    return copy_for_each(value, axis).max(axis=0)


def cut_along(value, dim, devices):
    dims = value.shape
    blocks = value.reshape(*dims[:dim], devices, dims[dim] // devices, *dims[dim + 1 :])
    return jnp.moveaxis(blocks, dim, 0)


def sent_and_summed(value, axis, dim):
    blocks = cut_along(value, dim, lax.axis_size(axis))
    arrived = lax.all_to_all(blocks, axis, split_axis=0, concat_axis=0, tiled=True)
    return arrived.sum(axis=0)


def sent_together(arrays, axis, dim, along):
    widths = [math.prod(a.shape[along:]) for a in arrays]
    both = jnp.concatenate(
        [a.reshape(*a.shape[:along], w) for a, w in zip(arrays, widths)], axis=along
    )
    result = sent_and_summed(both, axis, dim)
    blocks = jnp.split(result, [sum(widths[:k]) for k in range(1, len(widths))], axis=along)
    return tuple(
        (b.reshape(*result.shape[:along], *a.shape[along:]) for a, b in zip(arrays, blocks))
    )


def joined_along(blocks, dim):
    blocks = jnp.moveaxis(blocks, 0, dim)
    dims = blocks.shape
    return blocks.reshape(*dims[:dim], dims[dim] * dims[dim + 1], *dims[dim + 2 :])


def collect(value, axis, dim):
    return joined_along(copy_for_each(value, axis), dim)


def rotate(queries, positions):
    half_rope = ROPE // 2
    frequency = theta ** (-2.0 * jnp.arange(half_rope, dtype=jnp.float32) / ROPE)
    angles = positions.astype(jnp.float32)[..., None] * frequency
    cosine = jnp.cos(angles)[..., None, :]
    sine_part = jnp.sin(angles)[..., None, :]
    front_half = queries[..., LATENT : LATENT + half_rope].astype(jnp.float32)
    back_half = queries[..., LATENT + half_rope :].astype(jnp.float32)
    turned = jnp.concatenate(
        [front_half * cosine - back_half * sine_part, back_half * cosine + front_half * sine_part],
        axis=-1,
    )
    return jnp.concatenate([queries[..., :LATENT], turned.astype(jnp.bfloat16)], axis=-1)


def score_rows(blocks, limits, cache_rows, first_place):
    scores = lax.dot_general(
        blocks, cache_rows, (((1,), (1,)), ((), ())), preferred_element_type=jnp.float32
    ) * (NOPE + ROPE) ** (-0.5)
    places = first_place + jnp.arange(cache_rows.shape[0], dtype=jnp.int32)
    visible = places[None, :] <= limits[:, None]
    return (scores, visible)


def per_device(queries, cache, lengths, offsets, w_uv, w_out):
    head_count = queries.shape[2]
    entries = queries.shape[3]
    positions = lengths[0] - DRAFT + offsets[0]
    rotated = rotate(queries[0], positions)
    cache_rows = cache[0]
    values = cache_rows[:, :LATENT]
    first_place = lax.axis_index("ctx") * cache_rows.shape[0]
    devices_ctx = lax.axis_size("ctx")
    blocks = rotated.reshape(DRAFT * head_count, entries)
    gathered = lax.all_gather(blocks, "ctx", axis=0, tiled=True)
    limits = jnp.tile(jnp.repeat(positions, head_count), devices_ctx)
    scores, visible = score_rows(gathered, limits, cache_rows, first_place)
    maxima = jnp.max(jnp.where(visible, scores, negative), axis=1)
    peaks = taken_together(maxima, "ctx")
    weights = jnp.where(visible, jnp.exp(scores - peaks[:, None]), 0.0)
    totals = jnp.sum(weights, axis=1)
    numerators = jnp.dot(weights.astype(jnp.bfloat16), values, preferred_element_type=jnp.float32)
    numerators, totals = sent_together((numerators, totals), "ctx", 0, 1)
    attended = (
        (numerators / totals[:, None]).astype(jnp.bfloat16).reshape(DRAFT, head_count, LATENT)
    )
    head_values = jnp.einsum(
        "thl,hlv->thv", attended, w_uv, preferred_element_type=jnp.float32
    ).astype(jnp.bfloat16)
    head_values = head_values.reshape(DRAFT, head_count * head_values.shape[2])
    every_token = collect(head_values, "seq", 0)
    return sent_and_summed(
        jnp.dot(every_token, w_out, preferred_element_type=jnp.float32), ("ctx", "head"), 0
    ).astype(jnp.bfloat16)


def solution(mesh):
    in_specs = (
        P(("groups", "seq"), None, ("ctx", "head"), None),
        P(("groups", "seq"), "ctx", None),
        P(("groups", "seq")),
        P(("groups", "seq"), None),
        P(("ctx", "head"), None, None),
        P(("ctx", "head"), "seq"),
    )
    out_specs = P(("groups", "ctx", "head"), "seq")
    return jax.shard_map(
        per_device, mesh=mesh, in_specs=in_specs, out_specs=out_specs, check_vma=False
    )
```

profile of v0, /device:TPU:80, one launch (start us, length us, event | category | flops | bytes accessed | tf_op | source)
XLA Modules:
  0.0 169.3 jit_solution(17803864457834293212)
XLA Ops:
  0.0 0.0 copy-start
  0.7 0.7 fusion.19
  1.4 0.1 broadcast_in_dim.15
  1.5 0.1 tile.7
  1.6 0.1 le.16
  1.7 0.7 slice.16
  2.4 0.1 multiply_cosine_fusion
  2.5 0.8 fusion.14
  3.3 0.1 pad_maximum_fusion.1
  3.4 69.8 %all_gather.3 = bf16[256,576]{1,0:T(8,128)(2,1)S(1)} all-gather(bf16[16,576]{1,0:T(8,128)(2,1)S(1)} %reshape.103), channel_id=1, replica_groups=mesh['groups'=2,'ctx'=16,'seq'=8,'head'=2] {'ctx'}, dimensions={0}, use_global_device_ids=true | all-gather | bytes 313344 | tf_op jit(solution)/shard_map/all_gather | solution.py:94
  73.3 5.2 %fusion = (f32[256]{0:T(256)S(1)}, f32[256,3072]{1,0:T(8,128)}) fusion(s32[3072]{0:T(1024)S(1)} %iota_add_fusion, s32[256]{0:T(256)S(1)} %le.16, bf16[256,576]{1,0:T(8,128)(2,1)S(1)} %all_gather.3, bf16[1,3072,576]{1,2,0:T(8,128)(2,1)} %param.7), kind=kOutput, calls=%fused_computation.3 | convolution fusion | flops 909115136 | bytes 6993920 | tf_op jit(solution)/shard_map/dot_general | solution.py:76
  78.5 15.5 %all_to_all.21 = f32[16,1,256]{2,1,0:T(1,128)S(1)} all-to-all(f32[16,1,256]{2,1,0:T(1,128)S(1)} %broadcast_in_dim.31), channel_id=1, replica_groups=mesh['groups'=2,'ctx'=16,'seq'=8,'head'=2] {'ctx'}, dimensions={0} | all-to-all | bytes 32768 | tf_op jit(solution)/shard_map/all_to_all | solution.py:17
  94.0 0.0 copy-start.1
  94.0 2.8 %fusion.3 = f32[256]{0:T(256)S(1)} fusion(f32[256,3072]{1,0:T(8,128)} %get-tuple-element.12, f32[256]{0:T(256)S(1)} %reduce_max.19, s32[3072]{0:T(1024)S(1)} %iota_add_fusion, s32[256]{0:T(256)S(1)} %le.16), kind=kLoop, calls=%fused_computation.6 | loop fusion | flops 3145472 | bytes 3161088 | tf_op jit(solution)/shard_map/reduce_sum | solution.py:100
  96.8 0.0 copy-done.1
  96.8 3.0 %fusion.1 = f32[256,512]{1,0:T(8,128)S(1)} fusion(bf16[3072,576]{0,1:T(8,128)(2,1)} %bitcast.24, f32[256,3072]{1,0:T(8,128)S(1)} %copy-done.1, f32[256]{0:T(256)S(1)} %reduce_max.19, s32[3072]{0:T(1024)S(1)} %iota_add_fusion, s32[256]{0:T(256)S(1)} %le.16), kind=kOutput, calls=%fused_computation.4 | convolution fusion | flops 808452096 | bytes 6830080 | tf_op jit(solution)/shard_map/dot_general | solution.py:101
  99.8 0.0 copy-start.2
  99.8 0.2 concatenate.18
  100.0 0.1 pad_maximum_fusion
  100.1 31.9 %all_to_all.22 = f32[16,16,513]{2,1,0:T(8,128)S(1)} all-to-all(f32[16,16,513]{2,1,0:T(8,128)S(1)} %pad_maximum_fusion), channel_id=1, replica_groups=mesh['groups'=2,'ctx'=16,'seq'=8,'head'=2] {'ctx'}, dimensions={0} | all-to-all | bytes 1050624 | tf_op jit(solution)/shard_map/all_to_all | solution.py:34
  132.1 0.1 slice_reduce_fusion
  132.2 0.1 fusion.11
  132.3 0.0 copy-done.2
  132.3 0.2 fusion.10
  132.5 15.1 %all_to_all.23 = bf16[8,4,512]{2,1,0:T(4,128)(2,1)S(1)} all-to-all(bf16[8,4,512]{2,1,0:T(4,128)(2,1)S(1)} %broadcast_in_dim.34), channel_id=1, replica_groups=mesh['groups'=2,'ctx'=16,'seq'=8,'head'=2] {'seq'}, dimensions={0} | all-to-all | bytes 65536 | tf_op jit(solution)/shard_map/all_to_all | solution.py:17
  147.6 0.0 copy-done
  147.7 0.3 convolution_bitcast_fusion
  147.9 0.1 copy.21
  148.1 20.6 %all_to_all.24 = f32[32,1,896]{2,1,0:T(1,128)S(1)} all-to-all(f32[32,1,896]{2,1,0:T(1,128)S(1)} %copy.21), channel_id=1, replica_groups=mesh['groups'=2,'ctx'=16,'seq'=8,'head'=2] {'ctx','head'}, dimensions={0} | all-to-all | bytes 229376 | tf_op jit(solution)/shard_map/all_to_all | solution.py:34
  168.7 0.1 reduce_sum.29
  168.8 0.6 convert_element_type.48
  (10 shorter events, 0.2 us)
Async XLA Ops:
  0.0 147.6 %copy-start = (bf16[512,896]{1,0:T(8,128)(2,1)S(1)}, bf16[512,896]{1,0:T(8,128)(2,1)}, u32[]{:S(2)}) copy-start(bf16[512,896]{1,0:T(8,128)(2,1)} %param.11) | copy-start | bytes 2752516
  94.0 2.8 %copy-start.1 = (f32[256,3072]{1,0:T(8,128)S(1)}, f32[256,3072]{1,0:T(8,128)}, u32[]{:S(2)}) copy-start(f32[256,3072]{1,0:T(8,128)} %get-tuple-element.12) | copy-start | bytes 9437188
  99.8 32.5 %copy-start.2 = (bf16[4,512,128]{2,1,0:T(8,128)(2,1)S(1)}, bf16[4,512,128]{2,1,0:T(8,128)(2,1)}, u32[]{:S(2)}) copy-start(bf16[4,512,128]{2,1,0:T(8,128)(2,1)} %param.10) | copy-start | bytes 1572868
where the time goes:
time: 170 us; the launch traced here: 169 us
  blocking collectives  153 us (90%)
  matrix products  8.6 us (5%)
  other arithmetic  4.82 us (3%)
  local copies, waits for them, and re-layouts  2.13 us (1%)
    all_gather x1, blocking collectives, per_device(): gathered = lax.all_gather(blocks, 'ctx', axis=0, tiled=True)  69.8 us
    all_to_all x2, blocking collectives, sent_and_summed(): lax.all_to_all(blocks, axis, split_axis=0, concat_axis=0, tiled=True)  52.5 us
    all_to_all x2, blocking collectives, copy_for_each(): lax.all_to_all(jnp.broadcast_to(value[None], (devices, *value.shape)), ax...  30.6 us
    dot_general x1, matrix products, score_rows(): lax.dot_general(blocks, cache_rows, (((1,), (1,)), ((), ())), preferred_e...  5.18 us

commit v1 on v0

--- a/solution.py
+++ b/solution.py
@@ -10,6 +10,12 @@
 DRAFT = 4
 theta = 10000.0
 negative = -1e30
+
+
+def gather_by_exchange(x, axis, dim):
+    devices = lax.axis_size(axis)
+    repeats = [devices if d == dim else 1 for d in range(x.ndim)]
+    return lax.all_to_all(jnp.tile(x, repeats), axis, split_axis=dim, concat_axis=dim, tiled=True)
 
 
 def copy_for_each(value, axis):
@@ -91,7 +97,7 @@
     first_place = lax.axis_index("ctx") * cache_rows.shape[0]
     devices_ctx = lax.axis_size("ctx")
     blocks = rotated.reshape(DRAFT * head_count, entries)
-    gathered = lax.all_gather(blocks, "ctx", axis=0, tiled=True)
+    gathered = gather_by_exchange(blocks, "ctx", 0)
     limits = jnp.tile(jnp.repeat(positions, head_count), devices_ctx)
     scores, visible = score_rows(gathered, limits, cache_rows, first_place)
     maxima = jnp.max(jnp.where(visible, scores, negative), axis=1)

time: 170 us -> 174 us (1.024)
  blocking collectives: 153 us -> 92.5 us
  starting transfers between devices: 0 us -> 43.7 us
  waiting for transfers between devices: 0 us -> 20.5 us
    all_gather x1 -> x0, blocking collectives: 69.8 us -> none  [per_device(): gathered = lax.all_gather(blocks, 'ctx', axis=0, tiled=True)]
    all_to_all x0 -> x1, starting transfers between devices: none -> 43.7 us  [gather_by_exchange(): lax.all_to_all(jnp.tile(x, repeats), axis, split_axis=dim, concat_axis=di...]
    all_to_all x0 -> x1, waiting for transfers between devices: none -> 20.5 us  [gather_by_exchange(): lax.all_to_all(jnp.tile(x, repeats), axis, split_axis=dim, concat_axis=di...]
    all_to_all x2, blocking collectives: 52.5 us -> 59 us  [sent_and_summed(): lax.all_to_all(blocks, axis, split_axis=0, concat_axis=0, tiled=True)]
    all_to_all x2, blocking collectives: 30.6 us -> 33.5 us  [copy_for_each(): lax.all_to_all(jnp.broadcast_to(value[None], (devices, *value.shape)), ax...]
  transfers between devices with their start and end apart: 0 -> 1, of which waited for: 0 -> 1; matrix products, arithmetic and copies ran while one was open for 0% -> 0% of each run, Pallas kernels for 0% -> 0%
where the time goes in v1:
time: 174 us
  blocking collectives  92.5 us (53%)
  starting transfers between devices  43.7 us (25%)
  waiting for transfers between devices  20.5 us (12%)
  matrix products  8.65 us (5%)
  other arithmetic  4.82 us (3%)
  local copies, waits for them, and re-layouts  2.86 us (2%)
    all_to_all x2, blocking collectives, sent_and_summed(): lax.all_to_all(blocks, axis, split_axis=0, concat_axis=0, tiled=True)  59 us
    all_to_all x1, starting transfers between devices, gather_by_exchange(): lax.all_to_all(jnp.tile(x, repeats), axis, split_axis=dim, concat_axis=di...  43.7 us
    all_to_all x2, blocking collectives, copy_for_each(): lax.all_to_all(jnp.broadcast_to(value[None], (devices, *value.shape)), ax...  33.5 us
    all_to_all x1, waiting for transfers between devices, gather_by_exchange(): lax.all_to_all(jnp.tile(x, repeats), axis, split_axis=dim, concat_axis=di...  20.5 us
    dot_general x1, matrix products, score_rows(): lax.dot_general(blocks, cache_rows, (((1,), (1,)), ((), ())), preferred_e...  5.23 us
  transfers between devices with their start and end apart: 1, of which 1 were waited for; matrix products, arithmetic and copies ran while one was open for 0% of the time, Pallas kernels for 0%

profile of v1, /device:TPU:80, one launch (start us, length us, event | category | flops | bytes accessed | tf_op | source)
XLA Modules:
  0.0 173.9 jit_solution(9925113017237754606)
XLA Ops:
  0.0 0.0 copy-start
  0.7 0.7 slice.16
  1.5 0.7 fusion.19
  2.1 0.1 multiply_cosine_fusion
  2.2 0.8 fusion.14
  3.1 0.1 pad_maximum_fusion.1
  3.2 0.7 tile.18
  3.9 43.7 %all-to-all-start = ((bf16[16,16,576]{2,1,0:T(8,128)(2,1)}), bf16[16,16,576]{2,1,0:T(8,128)(2,1)S(1)}, u32[]{:S(2)}, u32[]{:S(2)}) async-start(bf16[16,16,576]{2,1,0:T(8,128)(2,1)} %tile.18), calls=%async_computation | async-start | bytes 655360 | tf_op jit(solution)/shard_map/all_to_all | solution.py:18
  47.6 0.1 broadcast_in_dim.15
  47.7 0.1 tile.15
  47.8 0.1 le.16
  47.9 20.5 %all-to-all-done = bf16[16,16,576]{2,1,0:T(8,128)(2,1)S(1)} async-done(((bf16[16,16,576]{2,1,0:T(8,128)(2,1)}), bf16[16,16,576]{2,1,0:T(8,128)(2,1)S(1)}, u32[]{:S(2)}, u32[]{:S(2)}) %all-to-all-start) | async-done | bytes 294944 | tf_op jit(solution)/shard_map/all_to_all | solution.py:18
  68.4 5.2 %fusion = (f32[256]{0:T(256)S(1)}, f32[256,3072]{1,0:T(8,128)}) fusion(s32[3072]{0:T(1024)S(1)} %iota_add_fusion, s32[256]{0:T(256)S(1)} %le.16, bf16[256,576]{1,0:T(8,128)(2,1)S(1)} %bitcast.23, bf16[1,3072,576]{1,2,0:T(8,128)(2,1)} %param.7), kind=kOutput, calls=%fused_computation.3 | convolution fusion | flops 909115136 | bytes 6993920 | tf_op jit(solution)/shard_map/dot_general | solution.py:82
  73.7 18.4 %all_to_all.30 = f32[16,1,256]{2,1,0:T(1,128)S(1)} all-to-all(f32[16,1,256]{2,1,0:T(1,128)S(1)} %broadcast_in_dim.31), channel_id=1, replica_groups=mesh['groups'=2,'ctx'=16,'seq'=8,'head'=2] {'ctx'}, dimensions={0} | all-to-all | bytes 32768 | tf_op jit(solution)/shard_map/all_to_all | solution.py:23
  92.1 0.0 copy-start.1
  92.1 2.8 %fusion.3 = f32[256]{0:T(256)S(1)} fusion(f32[256,3072]{1,0:T(8,128)} %get-tuple-element.12, f32[256]{0:T(256)S(1)} %reduce_max.19, s32[3072]{0:T(1024)S(1)} %iota_add_fusion, s32[256]{0:T(256)S(1)} %le.16), kind=kLoop, calls=%fused_computation.6 | loop fusion | flops 3145472 | bytes 3161088 | tf_op jit(solution)/shard_map/reduce_sum | solution.py:106
  94.9 0.0 copy-done.1
  94.9 3.0 %fusion.1 = f32[256,512]{1,0:T(8,128)S(1)} fusion(bf16[3072,576]{0,1:T(8,128)(2,1)} %bitcast.26, f32[256,3072]{1,0:T(8,128)S(1)} %copy-done.1, f32[256]{0:T(256)S(1)} %reduce_max.19, s32[3072]{0:T(1024)S(1)} %iota_add_fusion, s32[256]{0:T(256)S(1)} %le.16), kind=kOutput, calls=%fused_computation.4 | convolution fusion | flops 808452096 | bytes 6830080 | tf_op jit(solution)/shard_map/dot_general | solution.py:107
  97.9 0.0 copy-start.2
  97.9 0.2 concatenate.18
  98.1 0.1 pad_maximum_fusion
  98.2 38.3 %all_to_all.31 = f32[16,16,513]{2,1,0:T(8,128)S(1)} all-to-all(f32[16,16,513]{2,1,0:T(8,128)S(1)} %pad_maximum_fusion), channel_id=1, replica_groups=mesh['groups'=2,'ctx'=16,'seq'=8,'head'=2] {'ctx'}, dimensions={0} | all-to-all | bytes 1050624 | tf_op jit(solution)/shard_map/all_to_all | solution.py:40
  136.5 0.1 slice_reduce_fusion
  136.6 0.1 fusion.11
  136.7 0.0 copy-done.2
  136.8 0.2 fusion.10
  137.0 15.2 %all_to_all.32 = bf16[8,4,512]{2,1,0:T(4,128)(2,1)S(1)} all-to-all(bf16[8,4,512]{2,1,0:T(4,128)(2,1)S(1)} %broadcast_in_dim.34), channel_id=1, replica_groups=mesh['groups'=2,'ctx'=16,'seq'=8,'head'=2] {'seq'}, dimensions={0} | all-to-all | bytes 65536 | tf_op jit(solution)/shard_map/all_to_all | solution.py:23
  152.1 0.0 copy-done
  152.1 0.3 convolution_bitcast_fusion
  152.4 0.1 copy.21
  152.5 20.7 %all_to_all.33 = f32[32,1,896]{2,1,0:T(1,128)S(1)} all-to-all(f32[32,1,896]{2,1,0:T(1,128)S(1)} %copy.21), channel_id=1, replica_groups=mesh['groups'=2,'ctx'=16,'seq'=8,'head'=2] {'ctx','head'}, dimensions={0} | all-to-all | bytes 229376 | tf_op jit(solution)/shard_map/all_to_all | solution.py:40
  173.2 0.1 reduce_sum.29
  173.3 0.6 convert_element_type.48
  (10 shorter events, 0.2 us)
Async XLA Ops:
  0.0 152.1 %copy-start = (bf16[512,896]{1,0:T(8,128)(2,1)S(1)}, bf16[512,896]{1,0:T(8,128)(2,1)}, u32[]{:S(2)}) copy-start(bf16[512,896]{1,0:T(8,128)(2,1)} %param.11) | copy-start | bytes 2752516
  3.9 64.5 %all-to-all-start = ((bf16[16,16,576]{2,1,0:T(8,128)(2,1)}), bf16[16,16,576]{2,1,0:T(8,128)(2,1)S(1)}, u32[]{:S(2)}, u32[]{:S(2)}) async-start(bf16[16,16,576]{2,1,0:T(8,128)(2,1)} %tile.18), calls=%async_computation | async-start | bytes 655360 | tf_op jit(solution)/shard_map/all_to_all | solution.py:18
  92.1 2.8 %copy-start.1 = (f32[256,3072]{1,0:T(8,128)S(1)}, f32[256,3072]{1,0:T(8,128)}, u32[]{:S(2)}) copy-start(f32[256,3072]{1,0:T(8,128)} %get-tuple-element.12) | copy-start | bytes 9437188
  97.9 38.9 %copy-start.2 = (bf16[4,512,128]{2,1,0:T(8,128)(2,1)S(1)}, bf16[4,512,128]{2,1,0:T(8,128)(2,1)}, u32[]{:S(2)}) copy-start(bf16[4,512,128]{2,1,0:T(8,128)(2,1)} %param.10) | copy-start | bytes 1572868
